TPU v7x, 32 devices: a whole 2x2x4 slice. The times are simulated.
32 devices in a mesh: row: 8 (over y, x, core), col: 4 (over z).
Axes of the slice: x: 2, y: 2, z: 4, core: 2. Of those that a mesh axis runs over, the one named last changes fastest.
Arguments:
- temps: bfloat16 [12, 64, 16384], P(None, None, ('row', 'col')), may hold values from -6 to 6
- sensors: int32 [12, 512], replicated, may hold values from 0 to 16383
Outputs:
- corr: bfloat16 [512, 16384], P('col', 'row')
Inputs may be any that keep to these rules, and one draw needn't show every extreme that they name: `sensors`: each entry is a pixel index of its tier; candidates may repeat.
All inputs are finite; a program needn't handle non-finite values.
Results may differ from a plain program's by a relative error of at most 0.001.
Values may be sent and summed in bfloat16 or wider, within the bound.
A program may use at most 64 MiB of HBM per device.

v0:
```python
import jax
import jax.numpy as jnp
from jax import lax
from jax.sharding import PartitionSpec as P


def select_columns(fields, sensor_rows, first_pixel):
    width = fields.shape[2]
    offsets = sensor_rows - first_pixel
    pixel_ids = lax.broadcasted_iota(jnp.int32, (width, sensor_rows.shape[1]), 0)

    def one_tier(pair):
        tier_fields, tier_offsets = pair
        selector = (pixel_ids == tier_offsets[None, :]).astype(jnp.bfloat16)
        return jnp.dot(tier_fields, selector, preferred_element_type=jnp.float32)

    return lax.map(one_tier, (fields, offsets))


def body(temps, sensors):
    col_count = lax.axis_size("col")
    first_pixel = (lax.axis_index("row") * col_count + lax.axis_index("col")) * temps.shape[2]
    local_values = select_columns(temps, sensors, first_pixel)
    owned = lax.psum_scatter(
        local_values.astype(jnp.bfloat16), "col", scatter_dimension=2, tiled=True
    )
    readings = lax.psum(owned, "row").astype(jnp.float32).astype(jnp.bfloat16)
    scale_factor = 1.0 / jnp.sqrt(jnp.float32(temps.shape[0] * temps.shape[1]))
    summed = jnp.einsum(
        "tsc,tsp->cp",
        lax.all_gather(readings, "col", axis=2, tiled=True),
        temps,
        preferred_element_type=jnp.float32,
    )
    rounded = (summed * scale_factor).astype(jnp.bfloat16)
    return lax.all_to_all(rounded, "col", split_axis=0, concat_axis=1, tiled=True)


def solution(mesh):
    placed = (P(None, None, ("row", "col")), P())
    return jax.shard_map(
        body, mesh=mesh, in_specs=placed, out_specs=P("col", "row"), check_vma=False
    )
```

profile of v0, /device:TPU:0, one launch (start us, length us, event | category | flops | bytes accessed | tf_op | source)
XLA Modules:
  0.0 149.4 jit_solution(5405462871860880620)
XLA Ops:
  6.5 0.8 broadcast_subtract_fusion
  7.3 14.2 %while.11 = (s32[]{:T(128)}, bf16[12,64,512]{2,1,0:T(8,128)(2,1)S(1)}, bf16[12,64,512]{2,1,0:T(8,128)(2,1)}, s32[12,512]{1,0:T(8,128)S(1)}, s32[]{:T(128)}) while((s32[]{:T(128)}, bf16[12,64,512]{2,1,0:T(8,128)(2,1)S(1)}, bf16[12,64,512]{2,1,0:T(8,128)(2,1)}, s32[12,512]{1,0:T(8,128)S(1)}, s32[]{:T(128)}) %tuple.21), condition=%wide.region_1.2_spmd.clone, body=%wide.region_0.1_spmd.clone.sunk | while | flops 33816576 | bytes 203849 | solution.py:17
  7.3 1.2 fusion.14
  8.5 1.2 fusion.14
  9.7 1.2 fusion.14
  10.9 1.2 fusion.14
  12.1 1.2 fusion.14
  13.2 1.2 fusion.14
  14.4 1.2 fusion.14
  15.6 1.2 fusion.14
  16.8 1.2 fusion.14
  18.0 1.2 fusion.14
  19.2 1.2 fusion.14
  20.4 1.2 fusion.14
  21.5 2.0 %copy.5 = bf16[12,64,512]{1,0,2:T(8,128)(2,1)S(1)} copy(bf16[12,64,512]{2,1,0:T(8,128)(2,1)S(1)} %get-tuple-element.32) | data formatting | bytes 1572864
  23.5 2.0 %reshape.4 = bf16[512,768]{1,0:T(8,128)(2,1)} reshape(bf16[512,12,64]{2,1,0:T(8,128)(2,1)S(1)} %bitcast.28) | data formatting | bytes 1572864
  25.7 26.0 %reduce-scatter.4.cloned.1.call-done = bf16[128,768]{1,0:T(8,128)(2,1)} async-done(((bf16[512,768]{1,0:T(8,128)(2,1)}), bf16[128,768]{1,0:T(8,128)(2,1)}) %reduce-scatter.4.cloned.1.call-update) | async-done | bytes 196624
  51.7 1.3 reshape.5
  52.9 1.0 copy.6
  54.0 53.9 %all-reduce.2.cloned.1.call-done = bf16[12,64,128]{2,1,0:T(8,128)(2,1)} async-done(((bf16[12,64,128]{2,1,0:T(8,128)(2,1)}), bf16[12,64,128]{2,1,0:T(8,128)(2,1)}) %all-reduce.2.cloned.1.call-update) | async-done | bytes 196624 | tf_op jit(solution)/shard_map/psum | solution.py:27
  107.9 18.8 %all_gather.3 = bf16[12,64,512]{2,1,0:T(8,128)(2,1)S(1)} all-gather(bf16[12,64,128]{2,1,0:T(8,128)(2,1)} %all-reduce.2.cloned.1.call-done), channel_id=1, replica_groups=mesh['row'=8,'col'=4] {'col'}, dimensions={2}, use_global_device_ids=true | all-gather | bytes 983040 | tf_op jit(solution)/shard_map/all_gather | solution.py:31
  126.7 0.6 fusion.8
  127.3 14.4 %all_to_all.19 = bf16[4,128,512]{2,1,0:T(8,128)(2,1)S(1)} all-to-all(bf16[4,128,512]{2,1,0:T(8,128)(2,1)S(1)} %bitcast.31), channel_id=1, replica_groups=mesh['row'=8,'col'=4] {'col'}, dimensions={0} | all-to-all | bytes 1048576 | tf_op jit(solution)/shard_map/all_to_all | solution.py:36
  141.8 0.8 copy.7
  (19 shorter events, 0.2 us)
Async XLA Ops:
  6.5 45.1 %reduce-scatter.4.cloned.1.call-start = ((), (), s32[]{:S(2)}) async-start(), calls=%async_computation.3 | async-start | bytes 983040
  25.6 101.2 %copy-start = (bf16[12,64,512]{2,1,0:T(8,128)(2,1)S(1)}, bf16[12,64,512]{2,1,0:T(8,128)(2,1)}, u32[]{:S(2)}) copy-start(bf16[12,64,512]{2,1,0:T(8,128)(2,1)} %get-tuple-element.99) | copy-start | bytes 2359300
  25.6 82.3 %all-reduce.2.cloned.1.call-start = ((), (), s32[]{:S(2)}) async-start(), calls=%async_computation.2 | async-start | bytes 393216 | tf_op jit(solution)/shard_map/psum | solution.py:27
Sparse Core Ops, SparseCore 0:
  25.7 25.8 reduce-scatter.3
  54.7 53.1 all-reduce.1
where the time goes:
time: 150 us; the launch traced here: 149 us
  waiting for transfers between devices  80 us (53%)
  blocking collectives  33.2 us (22%)
  matrix products  14.5 us (10%)
  between operations  13.4 us (9%)
  local copies, waits for them, and re-layouts  7.3 us (5%)
    psum x1, waiting for transfers between devices, body(): readings = lax.psum(owned, 'row').astype(jnp.float32).astype(jnp.bfloat16)  53.9 us
    unnamed x3, waiting for transfers between devices  26 us
    all_gather x1, blocking collectives, body(): lax.all_gather(readings, 'col', axis=2, tiled=True)  18.8 us
    all_to_all x1, blocking collectives, body(): lax.all_to_all(rounded, 'col', split_axis=0, concat_axis=1, tiled=True)  14.4 us
    dot_general x12, matrix products, one_tier(): return jnp.dot(tier_fields, selector, preferred_element_type=jnp.float32)  13.9 us
    unnamed x6, local copies, waits for them, and re-layouts  6.33 us
  transfers between devices with their start and end apart: 2, of which 2 were waited for; matrix products, arithmetic and copies ran while one was open for 0% of the time, Pallas kernels for 0%

commit v1 on v0

--- a/solution.py
+++ b/solution.py
@@ -2,6 +2,12 @@
 import jax.numpy as jnp
 from jax import lax
 from jax.sharding import PartitionSpec as P
+
+
+def in_order(pieces, dim):
+    pieces = jnp.moveaxis(pieces, 0, dim)
+    dims = pieces.shape
+    return pieces.reshape(*dims[:dim], dims[dim] * dims[dim + 1], *dims[dim + 2 :])
 
 
 def select_columns(fields, sensor_rows, first_pixel):
@@ -26,12 +32,26 @@
     )
     readings = lax.psum(owned, "row").astype(jnp.float32).astype(jnp.bfloat16)
     scale_factor = 1.0 / jnp.sqrt(jnp.float32(temps.shape[0] * temps.shape[1]))
-    summed = jnp.einsum(
-        "tsc,tsp->cp",
-        lax.all_gather(readings, "col", axis=2, tiled=True),
-        temps,
-        preferred_element_type=jnp.float32,
-    )
+    peers, index, width_2 = (lax.axis_size("col"), lax.axis_index("col"), readings.shape[2])
+    right = [(i, (i + 1) % peers) for i in range(peers)]
+    left = [(i, (i - 1) % peers) for i in range(peers)]
+    middle = peers // 2
+    pieces = {}
+    from_left = from_right = readings
+    for step in range(middle + 1):
+        next_left = lax.ppermute(from_left, "col", right) if step < middle else None
+        next_right = lax.ppermute(from_right, "col", left) if step < peers - middle - 1 else None
+        pieces[-step] = jnp.einsum(
+            "tsc,tsp->cp", from_left, temps, preferred_element_type=jnp.float32
+        )
+        if 0 < step < peers - middle:
+            pieces[step] = jnp.einsum(
+                "tsc,tsp->cp", from_right, temps, preferred_element_type=jnp.float32
+            )
+        from_left, from_right = (next_left, next_right)
+    pieces = jnp.stack([pieces[k] for k in sorted(pieces)])
+    pieces = pieces[(jnp.arange(peers) - index + middle) % peers]
+    summed = in_order(pieces, 0)
     rounded = (summed * scale_factor).astype(jnp.bfloat16)
     return lax.all_to_all(rounded, "col", split_axis=0, concat_axis=1, tiled=True)
 

time: 150 us -> 149 us (level)
  blocking collectives: 33.2 us -> 14.1 us
  waiting for transfers between devices: 80 us -> 91.5 us
  starting transfers between devices: 0.04 us -> 3.87 us
  matrix products: 14.5 us -> 16 us
    all_gather x1 -> x0, blocking collectives: 18.8 us -> none  [body(): lax.all_gather(readings, 'col', axis=2, tiled=True)]
    ppermute x0 -> x3, waiting for transfers between devices: none -> 11.6 us  [the longest x2 9.26 us: body(): next_left = lax.ppermute(from_left, 'col', right) if step < middle else None]
    ppermute x0 -> x3, starting transfers between devices: none -> 3.83 us  [the longest x1 2.34 us: body(): lax.ppermute(from_right, 'col', left)]
    dot_general x1 -> x4, matrix products: 0.6 us -> 2.12 us  [the longest x3 1.83 us: body(): jnp.einsum('tsc,tsp->cp', from_left, temps, preferred_element_type=jnp.fl...]
  transfers between devices with their start and end apart: 2 -> 5, of which waited for: 2 -> 5; matrix products, arithmetic and copies ran while one was open for 0% -> 1% of each run, Pallas kernels for 0% -> 0%
where the time goes in v1:
time: 149 us
  waiting for transfers between devices  91.5 us (61%)
  matrix products  16 us (11%)
  blocking collectives  14.1 us (9%)
  between operations  13.5 us (9%)
  local copies, waits for them, and re-layouts  8.36 us (6%)
  starting transfers between devices  3.87 us (3%)
    psum x1, waiting for transfers between devices, body(): readings = lax.psum(owned, 'row').astype(jnp.float32).astype(jnp.bfloat16)  53.9 us
    unnamed x3, waiting for transfers between devices  26 us
    all_to_all x1, blocking collectives, body(): lax.all_to_all(rounded, 'col', split_axis=0, concat_axis=1, tiled=True)  14.1 us
    dot_general x12, matrix products, one_tier(): return jnp.dot(tier_fields, selector, preferred_element_type=jnp.float32)  13.9 us
    ppermute x2, waiting for transfers between devices, body(): next_left = lax.ppermute(from_left, 'col', right) if step < middle else None  9.26 us
    unnamed x6, local copies, waits for them, and re-layouts  6.34 us
  transfers between devices with their start and end apart: 5, of which 5 were waited for; matrix products, arithmetic and copies ran while one was open for 1% of the time, Pallas kernels for 0%

profile of v1, /device:TPU:0, one launch (start us, length us, event | category | flops | bytes accessed | tf_op | source)
XLA Modules:
  0.0 148.6 jit_solution(5023286662475918888)
XLA Ops:
  7.3 14.2 %while.11 = (s32[]{:T(128)}, bf16[12,64,512]{2,1,0:T(8,128)(2,1)S(1)}, bf16[12,64,512]{2,1,0:T(8,128)(2,1)}, s32[12,512]{1,0:T(8,128)S(1)}, s32[]{:T(128)}) while((s32[]{:T(128)}, bf16[12,64,512]{2,1,0:T(8,128)(2,1)S(1)}, bf16[12,64,512]{2,1,0:T(8,128)(2,1)}, s32[12,512]{1,0:T(8,128)S(1)}, s32[]{:T(128)}) %tuple.21), condition=%wide.region_1.2_spmd.clone, body=%wide.region_0.1_spmd.clone.sunk | while | flops 33816576 | bytes 203841 | solution.py:23
  7.3 1.2 fusion.20
  8.5 1.2 fusion.20
  9.7 1.2 fusion.20
  10.9 1.2 fusion.20
  12.1 1.2 fusion.20
  13.2 1.2 fusion.20
  14.4 1.2 fusion.20
  15.6 1.2 fusion.20
  16.8 1.2 fusion.20
  18.0 1.2 fusion.20
  19.2 1.2 fusion.20
  21.5 2.0 %copy.7 = bf16[12,64,512]{1,0,2:T(8,128)(2,1)S(1)} copy(bf16[12,64,512]{2,1,0:T(8,128)(2,1)S(1)} %get-tuple-element.32) | data formatting | bytes 1572864
  23.6 2.0 %reshape.68 = bf16[512,768]{1,0:T(8,128)(2,1)} reshape(bf16[512,12,64]{2,1,0:T(8,128)(2,1)S(1)} %bitcast.40) | data formatting | bytes 1572864
  25.7 26.0 %reduce-scatter.4.cloned.1.call-done = bf16[128,768]{1,0:T(8,128)(2,1)} async-done(((bf16[512,768]{1,0:T(8,128)(2,1)}), bf16[128,768]{1,0:T(8,128)(2,1)}) %reduce-scatter.4.cloned.1.call-update) | async-done | bytes 196624
  51.7 1.3 reshape.69
  54.0 53.9 %all-reduce.2.cloned.1.call-done = bf16[12,64,128]{2,1,0:T(8,128)(2,1)} async-done(((bf16[12,64,128]{2,1,0:T(8,128)(2,1)}), bf16[12,64,128]{2,1,0:T(8,128)(2,1)}) %all-reduce.2.cloned.1.call-update) | async-done | bytes 196624 | tf_op jit(solution)/shard_map/psum | solution.py:33
  107.9 1.5 %collective-permute-start = (bf16[12,64,128]{2,1,0:T(8,128)(2,1)}, bf16[12,64,128]{2,1,0:T(8,128)(2,1)S(1)}, u32[]{:S(2)}, u32[]{:S(2)}) collective-permute-start(bf16[12,64,128]{2,1,0:T(8,128)(2,1)} %all-reduce.2.cloned.1.call-done), channel_id=1, source_target_pairs={{0,1},{1,2},{2,3},{3,0},{4,5},{5,6},{6,7},{7,4},{8,9},{9,10},{10,1... | collective-permute-start | bytes 589832 | tf_op jit(solution)/shard_map/ppermute | solution.py:42
  109.4 2.3 %collective-permute-start.2 = (bf16[12,64,128]{2,1,0:T(8,128)(2,1)}, bf16[12,64,128]{2,1,0:T(8,128)(2,1)S(1)}, u32[]{:S(2)}, u32[]{:S(2)}) collective-permute-start(bf16[12,64,128]{2,1,0:T(8,128)(2,1)} %all-reduce.2.cloned.1.call-done), channel_id=1, source_target_pairs={{0,3},{1,0},{2,1},{3,2},{4,7},{5,4},{6,5},{7,6},{8,11},{9,8},{10,9... | collective-permute-start | bytes 589832 | tf_op jit(solution)/shard_map/ppermute | solution.py:43
  111.8 1.2 convolution_bitcast_fusion.2
  113.0 4.7 %collective-permute-done = bf16[12,64,128]{2,1,0:T(8,128)(2,1)S(1)} collective-permute-done((bf16[12,64,128]{2,1,0:T(8,128)(2,1)}, bf16[12,64,128]{2,1,0:T(8,128)(2,1)S(1)}, u32[]{:S(2)}, u32[]{:S(2)}) %collective-permute-start) | collective-permute-done | bytes 196640 | tf_op jit(solution)/shard_map/ppermute | solution.py:42
  118.1 2.3 %collective-permute-done.2 = bf16[12,64,128]{2,1,0:T(8,128)(2,1)S(1)} collective-permute-done((bf16[12,64,128]{2,1,0:T(8,128)(2,1)}, bf16[12,64,128]{2,1,0:T(8,128)(2,1)S(1)}, u32[]{:S(2)}, u32[]{:S(2)}) %collective-permute-start.2) | collective-permute-done | bytes 196640 | tf_op jit(solution)/shard_map/ppermute | solution.py:43
  120.7 4.5 %collective-permute-done.1 = bf16[12,64,128]{2,1,0:T(8,128)(2,1)S(1)} collective-permute-done((bf16[12,64,128]{2,1,0:T(8,128)(2,1)S(1)}, bf16[12,64,128]{2,1,0:T(8,128)(2,1)S(1)}, u32[]{:S(2)}, u32[]{:S(2)}) %collective-permute-start.1) | collective-permute-done | bytes 196640 | tf_op jit(solution)/shard_map/ppermute | solution.py:42
  126.4 14.1 %all_to_all.16 = bf16[4,128,512]{2,1,0:T(8,128)(2,1)S(1)} all-to-all(bf16[4,128,512]{2,1,0:T(8,128)(2,1)S(1)} %multiply_convert_fusion), channel_id=1, replica_groups=mesh['row'=8,'col'=4] {'col'}, dimensions={0} | all-to-all | bytes 1048576 | tf_op jit(solution)/shard_map/all_to_all | solution.py:56
  (33 shorter events, 6.2 us)
Async XLA Ops:
  6.5 45.1 %reduce-scatter.4.cloned.1.call-start = ((), (), s32[]{:S(2)}) async-start(), calls=%async_computation.3 | async-start | bytes 983040
  23.5 88.2 %copy-start = (bf16[12,64,512]{2,1,0:T(8,128)(2,1)S(1)}, bf16[12,64,512]{2,1,0:T(8,128)(2,1)}, u32[]{:S(2)}) copy-start(bf16[12,64,512]{2,1,0:T(8,128)(2,1)} %get-tuple-element.93) | copy-start | bytes 2359300
  25.6 82.3 %all-reduce.2.cloned.1.call-start = ((), (), s32[]{:S(2)}) async-start(), calls=%async_computation.2 | async-start | bytes 393216 | tf_op jit(solution)/shard_map/psum | solution.py:33
  107.9 9.8 %collective-permute-start = (bf16[12,64,128]{2,1,0:T(8,128)(2,1)}, bf16[12,64,128]{2,1,0:T(8,128)(2,1)S(1)}, u32[]{:S(2)}, u32[]{:S(2)}) collective-permute-start(bf16[12,64,128]{2,1,0:T(8,128)(2,1)} %all-reduce.2.cloned.1.call-done), channel_id=1, source_target_pairs={{0,1},{1,2},{2,3},{3,0},{4,5},{5,6},{6,7},{7,4},{8,9},{9,10},{10,1... | collective-permute-start | bytes 589832 | tf_op jit(solution)/shard_map/ppermute | solution.py:42
  109.4 11.0 %collective-permute-start.2 = (bf16[12,64,128]{2,1,0:T(8,128)(2,1)}, bf16[12,64,128]{2,1,0:T(8,128)(2,1)S(1)}, u32[]{:S(2)}, u32[]{:S(2)}) collective-permute-start(bf16[12,64,128]{2,1,0:T(8,128)(2,1)} %all-reduce.2.cloned.1.call-done), channel_id=1, source_target_pairs={{0,3},{1,0},{2,1},{3,2},{4,7},{5,4},{6,5},{7,6},{8,11},{9,8},{10,9... | collective-permute-start | bytes 589832 | tf_op jit(solution)/shard_map/ppermute | solution.py:43
  117.8 7.5 %collective-permute-start.1 = (bf16[12,64,128]{2,1,0:T(8,128)(2,1)S(1)}, bf16[12,64,128]{2,1,0:T(8,128)(2,1)S(1)}, u32[]{:S(2)}, u32[]{:S(2)}) collective-permute-start(bf16[12,64,128]{2,1,0:T(8,128)(2,1)S(1)} %collective-permute-done), channel_id=1, source_target_pairs={{0,1},{1,2},{2,3},{3,0},{4,5},{5,6},{6,7},{7,4},{8,9},{9,10},{10,1... | collective-permute-start | bytes 589832 | tf_op jit(solution)/shard_map/ppermute | solution.py:42
Sparse Core Ops, SparseCore 0:
  25.7 25.8 reduce-scatter.3
  54.7 53.1 all-reduce.1

commit v2 on v0

--- a/solution.py
+++ b/solution.py
@@ -1,7 +1,20 @@
+import functools
 import jax
 import jax.numpy as jnp
 from jax import lax
 from jax.sharding import PartitionSpec as P
+from jax.lax import all_to_all, axis_size
+
+
+def fit_members_all_here(target, device_axis):
+    u_next = jnp.concatenate(
+        all_to_all(jnp.stack([target for _ in range(axis_size(device_axis))]), device_axis, 0, 0),
+        axis=2,
+    )
+    return u_next
+
+
+define_the_bars = functools.partial(fit_members_all_here, device_axis="col")
 
 
 def select_columns(fields, sensor_rows, first_pixel):
@@ -27,10 +40,7 @@
     readings = lax.psum(owned, "row").astype(jnp.float32).astype(jnp.bfloat16)
     scale_factor = 1.0 / jnp.sqrt(jnp.float32(temps.shape[0] * temps.shape[1]))
     summed = jnp.einsum(
-        "tsc,tsp->cp",
-        lax.all_gather(readings, "col", axis=2, tiled=True),
-        temps,
-        preferred_element_type=jnp.float32,
+        "tsc,tsp->cp", define_the_bars(readings), temps, preferred_element_type=jnp.float32
     )
     rounded = (summed * scale_factor).astype(jnp.bfloat16)
     return lax.all_to_all(rounded, "col", split_axis=0, concat_axis=1, tiled=True)

time: 150 us -> 158 us (1.053)
  blocking collectives: 33.2 us -> 40.2 us
    all_to_all x0 -> x1, blocking collectives: none -> 23.7 us  [fit_members_all_here(): all_to_all(jnp.stack([target for _ in range(axis_size(device_axis))]), de...]
    all_gather x1 -> x0, blocking collectives: 18.8 us -> none  [body(): lax.all_gather(readings, 'col', axis=2, tiled=True)]
    all_to_all x1, blocking collectives: 14.4 us -> 16.5 us  [body(): lax.all_to_all(rounded, 'col', split_axis=0, concat_axis=1, tiled=True)]
where the time goes in v2:
time: 158 us
  waiting for transfers between devices  80 us (51%)
  blocking collectives  40.2 us (25%)
  matrix products  14.5 us (9%)
  between operations  13.4 us (8%)
  local copies, waits for them, and re-layouts  8.4 us (5%)
    psum x1, waiting for transfers between devices, body(): readings = lax.psum(owned, 'row').astype(jnp.float32).astype(jnp.bfloat16)  53.9 us
    unnamed x3, waiting for transfers between devices  26 us
    all_to_all x1, blocking collectives, fit_members_all_here(): all_to_all(jnp.stack([target for _ in range(axis_size(device_axis))]), de...  23.7 us
    all_to_all x1, blocking collectives, body(): lax.all_to_all(rounded, 'col', split_axis=0, concat_axis=1, tiled=True)  16.5 us
    dot_general x12, matrix products, one_tier(): return jnp.dot(tier_fields, selector, preferred_element_type=jnp.float32)  13.9 us
    unnamed x6, local copies, waits for them, and re-layouts  6.34 us
  transfers between devices with their start and end apart: 2, of which 2 were waited for; matrix products, arithmetic and copies ran while one was open for 0% of the time, Pallas kernels for 0%

profile of v2, /device:TPU:0, one launch (start us, length us, event | category | flops | bytes accessed | tf_op | source)
XLA Modules:
  0.0 157.5 jit_solution(1605733432581588166)
XLA Ops:
  6.5 0.8 broadcast_subtract_fusion
  7.3 14.2 %while.11 = (s32[]{:T(128)}, bf16[12,64,512]{2,1,0:T(8,128)(2,1)S(1)}, bf16[12,64,512]{2,1,0:T(8,128)(2,1)}, s32[12,512]{1,0:T(8,128)S(1)}, s32[]{:T(128)}) while((s32[]{:T(128)}, bf16[12,64,512]{2,1,0:T(8,128)(2,1)S(1)}, bf16[12,64,512]{2,1,0:T(8,128)(2,1)}, s32[12,512]{1,0:T(8,128)S(1)}, s32[]{:T(128)}) %tuple.21), condition=%wide.region_1.2_spmd.clone, body=%wide.region_0.1_spmd.clone.sunk | while | flops 33816576 | bytes 203849 | solution.py:30
  7.3 1.2 fusion.16
  8.5 1.2 fusion.16
  9.7 1.2 fusion.16
  10.9 1.2 fusion.16
  12.1 1.2 fusion.16
  13.2 1.2 fusion.16
  14.4 1.2 fusion.16
  15.6 1.2 fusion.16
  16.8 1.2 fusion.16
  18.0 1.2 fusion.16
  19.2 1.2 fusion.16
  20.4 1.2 fusion.16
  21.5 2.0 %copy.6 = bf16[12,64,512]{1,0,2:T(8,128)(2,1)S(1)} copy(bf16[12,64,512]{2,1,0:T(8,128)(2,1)S(1)} %get-tuple-element.32) | data formatting | bytes 1572864
  23.5 2.0 %reshape.14 = bf16[512,768]{1,0:T(8,128)(2,1)} reshape(bf16[512,12,64]{2,1,0:T(8,128)(2,1)S(1)} %bitcast.35) | data formatting | bytes 1572864
  25.7 26.0 %reduce-scatter.4.cloned.1.call-done = bf16[128,768]{1,0:T(8,128)(2,1)} async-done(((bf16[512,768]{1,0:T(8,128)(2,1)}), bf16[128,768]{1,0:T(8,128)(2,1)}) %reduce-scatter.4.cloned.1.call-update) | async-done | bytes 196624
  51.7 1.3 reshape.15
  52.9 1.0 copy.7
  54.0 53.9 %all-reduce.2.cloned.1.call-done = bf16[12,64,128]{2,1,0:T(8,128)(2,1)} async-done(((bf16[12,64,128]{2,1,0:T(8,128)(2,1)}), bf16[12,64,128]{2,1,0:T(8,128)(2,1)}) %all-reduce.2.cloned.1.call-update) | async-done | bytes 196624 | tf_op jit(solution)/shard_map/psum | solution.py:40
  107.9 1.1 stack.2
  109.0 23.7 %all_to_all.24 = bf16[4,12,64,128]{3,2,1,0:T(8,128)(2,1)S(1)} all-to-all(bf16[4,12,64,128]{3,2,1,0:T(8,128)(2,1)S(1)} %stack.2), channel_id=1, replica_groups=mesh['row'=8,'col'=4] {'col'}, dimensions={0} | all-to-all | bytes 1572864 | tf_op jit(solution)/shard_map/all_to_all | solution.py:11
  133.3 16.5 %all_to_all.25 = bf16[4,128,512]{2,1,0:T(8,128)(2,1)S(1)} all-to-all(bf16[4,128,512]{2,1,0:T(8,128)(2,1)S(1)} %bitcast.38), channel_id=1, replica_groups=mesh['row'=8,'col'=4] {'col'}, dimensions={0} | all-to-all | bytes 1048576 | tf_op jit(solution)/shard_map/all_to_all | solution.py:46
  149.8 0.8 copy.9
  (20 shorter events, 0.8 us)
Async XLA Ops:
  6.5 45.1 %reduce-scatter.4.cloned.1.call-start = ((), (), s32[]{:S(2)}) async-start(), calls=%async_computation.4 | async-start | bytes 983040
  25.6 107.1 %copy-start = (bf16[12,64,512]{2,1,0:T(8,128)(2,1)S(1)}, bf16[12,64,512]{2,1,0:T(8,128)(2,1)}, u32[]{:S(2)}) copy-start(bf16[12,64,512]{2,1,0:T(8,128)(2,1)} %get-tuple-element.99) | copy-start | bytes 2359300
  25.6 82.3 %all-reduce.2.cloned.1.call-start = ((), (), s32[]{:S(2)}) async-start(), calls=%async_computation.3 | async-start | bytes 393216 | tf_op jit(solution)/shard_map/psum | solution.py:40
Sparse Core Ops, SparseCore 0:
  25.7 25.8 reduce-scatter.3
  54.7 53.1 all-reduce.1
